TPU v7x, 64 devices: a 2x2x8 block of a 4x4x8 slice. The times are simulated.
64 devices in a mesh: rep: 8 (over x, y, core), dp: 8 (over z).
Axes of the slice: x: 2, y: 2, z: 8, core: 2. Of those that a mesh axis runs over, the one named last changes fastest.
The devices are a block of a 4x4x8 slice.
Arguments:
- g_w_gate: bfloat16 [64, 2, 640, 1536], P(('rep', 'dp')), parts along dimension 0
- g_w_up: bfloat16 [64, 2, 640, 1536], P(('rep', 'dp')), parts along dimension 0
- g_w_down: bfloat16 [64, 2, 1536, 640], P(('rep', 'dp')), parts along dimension 0
- w_gate: bfloat16 [2, 640, 1536], replicated
- w_up: bfloat16 [2, 640, 1536], replicated
- w_down: bfloat16 [2, 1536, 640], replicated
- m_w_gate: float32 [2, 640, 1536], P(None, 'dp')
- m_w_up: float32 [2, 640, 1536], P(None, 'dp')
- m_w_down: float32 [2, 1536, 640], P(None, 'dp')
- v_w_gate: float32 [2, 640, 1536], P(None, 'dp')
- v_w_up: float32 [2, 640, 1536], P(None, 'dp')
- v_w_down: float32 [2, 1536, 640], P(None, 'dp')
Outputs:
- output 1: bfloat16 [16, 640, 1536], P('rep'), parts along dimension 0
- output 2: bfloat16 [16, 640, 1536], P('rep'), parts along dimension 0
- output 3: bfloat16 [16, 1536, 640], P('rep'), parts along dimension 0
- output 4: float32 [16, 640, 1536], P('rep', 'dp'), parts along dimension 0
- output 5: float32 [16, 640, 1536], P('rep', 'dp'), parts along dimension 0
- output 6: float32 [16, 1536, 640], P('rep', 'dp'), parts along dimension 0
- output 7: float32 [16, 640, 1536], P('rep', 'dp'), parts along dimension 0
- output 8: float32 [16, 640, 1536], P('rep', 'dp'), parts along dimension 0
- output 9: float32 [16, 1536, 640], P('rep', 'dp'), parts along dimension 0
There are 8 independent parts. A program takes and returns all parts, laid end to end along the dimension named above; an argument that names none is the same for every part.
All inputs are finite; a program needn't handle non-finite values.
Results may differ from a plain program's by a relative error of at most 0.022.
Values are sent between devices in bfloat16 or wider.
A program may use at most 768 MiB of HBM per device.

v0:
```python
import jax
import jax.numpy as jnp
from jax import lax
from jax.sharding import PartitionSpec as P


def adamw(w, m, v, g):
    m = 0.9 * m + 0.1 * g
    v = 0.95 * v + 0.05 * g * g
    step = m * lax.rsqrt(v + 1e-8) + 0.1 * w
    return (w - 0.02 * step).astype(jnp.bfloat16), m, v


def solution(mesh):
    def step(*arrays):
        terms, weights, m, v = (arrays[i : i + 3] for i in (0, 3, 6, 9))
        gradients = [lax.psum_scatter(t[0], "dp", scatter_dimension=1, tiled=True).astype(jnp.float32) for t in terms]
        me = lax.axis_index("dp")
        own = [lax.dynamic_slice_in_dim(w, me * one.shape[1], one.shape[1], 1).astype(jnp.float32) for w, one in zip(weights, m, strict=True)]
        new = [adamw(w, m, v, g) for w, m, v, g in zip(own, m, v, gradients, strict=True)]
        whole = [lax.all_gather(one[0], "dp", axis=1, tiled=True) for one in new]
        return (*whole, *(one[1] for one in new), *(one[2] for one in new))

    all_of, cut = P(None, None, None), P(None, "dp", None)
    return jax.shard_map(
        step,
        mesh=mesh,
        in_specs=(P(("rep", "dp"), None, None, None),) * 3 + (all_of,) * 3 + (cut,) * 6,
        out_specs=(P("rep", None, None),) * 3 + (P("rep", "dp", None),) * 6,
        check_vma=False,
    )
```

profile of v0, /device:TPU:22, one launch (start us, length us, event | category | flops | bytes accessed | tf_op | source)
XLA Modules:
  0.0 331.4 jit_solution(10154601214996839000)
XLA Ops:
  7.2 0.1 reduce-scatter.8.cloned.1.call-start
  7.3 0.7 reduce-scatter.8.cloned.1.call-update
  8.0 0.1 reduce-scatter.6.cloned.1.call-start
  8.1 0.7 reduce-scatter.6.cloned.1.call-update
  8.8 0.1 reduce-scatter.4.cloned.1.call-start
  8.9 0.7 reduce-scatter.4.cloned.1.call-update
  9.6 0.1 all-gather.8.cloned.1.call-start
  9.7 54.0 %reduce-scatter.8.cloned.1.call-done = bf16[2,192,640]{2,1,0:T(8,128)(2,1)} async-done(((bf16[2,1536,640]{2,1,0:T(8,128)(2,1)}), bf16[2,192,640]{2,1,0:T(8,128)(2,1)}) %reduce-scatter.8.cloned.1.call-update) | async-done | bytes 491536 | tf_op jit(solution)/shard_map/reduce_scatter | solution.py:17
  63.7 2.9 fusion.10
  66.6 0.1 all-gather.6.cloned.1.call-start
  66.7 47.9 %reduce-scatter.6.cloned.1.call-done = bf16[2,80,1536]{2,1,0:T(8,128)(2,1)} async-done(((bf16[2,640,1536]{2,1,0:T(8,128)(2,1)}), bf16[2,80,1536]{2,1,0:T(8,128)(2,1)}) %reduce-scatter.6.cloned.1.call-update) | async-done | bytes 491536 | tf_op jit(solution)/shard_map/reduce_scatter | solution.py:17
  114.6 3.2 fusion.6
  117.8 0.1 all-gather.6.cloned.1.call-update
  117.9 0.1 all-gather.4.cloned.1.call-start
  118.0 47.7 %reduce-scatter.4.cloned.1.call-done = bf16[2,80,1536]{2,1,0:T(8,128)(2,1)} async-done(((bf16[2,640,1536]{2,1,0:T(8,128)(2,1)}), bf16[2,80,1536]{2,1,0:T(8,128)(2,1)}) %reduce-scatter.4.cloned.1.call-update) | async-done | bytes 491536 | tf_op jit(solution)/shard_map/reduce_scatter | solution.py:17
  165.6 2.9 fusion.2
  168.5 0.1 all-gather.4.cloned.1.call-update
  168.6 47.0 %all-gather.8.cloned.1.call-done = bf16[2,1536,640]{2,1,0:T(8,128)(2,1)} async-done(((bf16[2,192,640]{2,1,0:T(8,128)(2,1)}), bf16[2,1536,640]{2,1,0:T(8,128)(2,1)}) %all-gather.8.cloned.1.call-update) | async-done | bytes 3932176 | tf_op jit(solution)/shard_map/all_gather | solution.py:21
  215.6 49.5 %all-gather.6.cloned.1.call-done = bf16[2,640,1536]{2,1,0:T(8,128)(2,1)} async-done(((bf16[2,80,1536]{2,1,0:T(8,128)(2,1)}), bf16[2,640,1536]{2,1,0:T(8,128)(2,1)}) %all-gather.6.cloned.1.call-update) | async-done | bytes 3932176 | tf_op jit(solution)/shard_map/all_gather | solution.py:21
  265.1 49.5 %all-gather.4.cloned.1.call-done = bf16[2,640,1536]{2,1,0:T(8,128)(2,1)} async-done(((bf16[2,80,1536]{2,1,0:T(8,128)(2,1)}), bf16[2,640,1536]{2,1,0:T(8,128)(2,1)}) %all-gather.4.cloned.1.call-update) | async-done | bytes 3932176 | tf_op jit(solution)/shard_map/all_gather | solution.py:21
  314.7 4.5 %copy.24 = bf16[2,640,1536]{2,1,0:T(8,128)(2,1)} copy(bf16[2,640,1536]{2,1,0:T(8,128)(2,1)} %all-gather.4.cloned.1.call-done) | data formatting | bytes 7864320
  319.1 2.0 copy.25
  321.1 1.5 copy-done
  322.7 1.9 copy.26
  (14 shorter events, 0.1 us)
Async XLA Ops:
  7.2 56.5 %reduce-scatter.8.cloned.1.call-start = ((), (), s32[]{:S(2)}) async-start(), calls=%async_computation.7 | async-start | bytes 4423680 | tf_op jit(solution)/shard_map/reduce_scatter | solution.py:17
  8.0 106.7 %reduce-scatter.6.cloned.1.call-start = ((), (), s32[]{:S(2)}) async-start(), calls=%async_computation.5 | async-start | bytes 4423680 | tf_op jit(solution)/shard_map/reduce_scatter | solution.py:17
  8.1 55.7 %copy-start.2 = (f32[2,192,640]{2,1,0:T(8,128)S(1)}, f32[2,192,640]{2,1,0:T(8,128)}, u32[]{:S(2)}) copy-start(f32[2,192,640]{2,1,0:T(8,128)} %param.23) | copy-start | bytes 2949124
  8.1 55.7 %copy-start.3 = (f32[2,192,640]{2,1,0:T(8,128)S(1)}, f32[2,192,640]{2,1,0:T(8,128)}, u32[]{:S(2)}) copy-start(f32[2,192,640]{2,1,0:T(8,128)} %param.20) | copy-start | bytes 2949124
  8.8 156.8 %reduce-scatter.4.cloned.1.call-start = ((), (), s32[]{:S(2)}) async-start(), calls=%async_computation.3 | async-start | bytes 4423680 | tf_op jit(solution)/shard_map/reduce_scatter | solution.py:17
  9.6 105.1 %copy-start.4 = (f32[2,80,1536]{2,1,0:T(8,128)S(1)}, f32[2,80,1536]{2,1,0:T(8,128)}, u32[]{:S(2)}) copy-start(f32[2,80,1536]{2,1,0:T(8,128)} %param.22) | copy-start | bytes 2949124
  9.6 206.0 %all-gather.8.cloned.1.call-start = ((), (), s32[]{:S(2)}) async-start(), calls=%async_computation.8 | async-start | bytes 4423680 | tf_op jit(solution)/shard_map/all_gather | solution.py:21
  66.6 99.1 %copy-start.5 = (f32[2,80,1536]{2,1,0:T(8,128)S(1)}, f32[2,80,1536]{2,1,0:T(8,128)}, u32[]{:S(2)}) copy-start(f32[2,80,1536]{2,1,0:T(8,128)} %param.21) | copy-start | bytes 2949124
  66.6 99.1 %copy-start.6 = (f32[2,80,1536]{2,1,0:T(8,128)S(1)}, f32[2,80,1536]{2,1,0:T(8,128)}, u32[]{:S(2)}) copy-start(f32[2,80,1536]{2,1,0:T(8,128)} %param.18) | copy-start | bytes 2949124
  66.6 198.5 %all-gather.6.cloned.1.call-start = ((), (), s32[]{:S(2)}) async-start(), calls=%async_computation.6 | async-start | bytes 4423680 | tf_op jit(solution)/shard_map/all_gather | solution.py:21
  117.9 196.8 %all-gather.4.cloned.1.call-start = ((), (), s32[]{:S(2)}) async-start(), calls=%async_computation.4 | async-start | bytes 4423680 | tf_op jit(solution)/shard_map/all_gather | solution.py:21
  314.7 4.5 %copy-start.1 = (bf16[2,640,1536]{2,1,0:T(8,128)(2,1)S(1)}, bf16[2,640,1536]{2,1,0:T(8,128)(2,1)}, u32[]{:S(2)}) copy-start(bf16[2,640,1536]{2,1,0:T(8,128)(2,1)} %all-gather.6.cloned.1.call-done) | copy-start | bytes 11796484
  319.1 3.5 %copy-start = (bf16[2,1536,640]{2,1,0:T(8,128)(2,1)S(1)}, bf16[2,1536,640]{2,1,0:T(8,128)(2,1)}, u32[]{:S(2)}) copy-start(bf16[2,1536,640]{2,1,0:T(8,128)(2,1)} %all-gather.8.cloned.1.call-done) | copy-start | bytes 11796484
Sparse Core Ops, SparseCore 0:
  10.4 53.2 reduce-scatter.7
  66.1 48.5 reduce-scatter.5
  117.0 48.5 reduce-scatter.3
  167.7 47.8 all-gather.7
  217.6 47.4 all-gather.5
  267.1 47.4 all-gather.3
where the time goes:
time: 332 us; the launch traced here: 331 us
  waiting for transfers between devices  298 us (90%)
  between operations  14.2 us (4%)
  local copies, waits for them, and re-layouts  9.93 us (3%)
  other arithmetic  8.94 us (3%)
    reduce_scatter x3, waiting for transfers between devices, step(): lax.psum_scatter(t[0], 'dp', scatter_dimension=1, tiled=True)  150 us
    all_gather x3, waiting for transfers between devices, step(): whole = [lax.all_gather(one[0], 'dp', axis=1, tiled=True) for one in new]  146 us
    unnamed x17, local copies, waits for them, and re-layouts  9.93 us
    convert_element_type x3, other arithmetic, adamw(): return ((w - 0.02 * step).astype(jnp.bfloat16), m, v)  8.94 us
  transfers between devices with their start and end apart: 6, of which 6 were waited for; matrix products, arithmetic and copies ran while one was open for 3% of the time, Pallas kernels for 0%

commit v1 on v0

v1 whole, which is shorter than its diff:
```python
import jax
import jax.numpy as jnp
from jax import lax
from jax.experimental import pallas as pl
from jax.experimental.pallas import tpu as pltpu
from jax.sharding import PartitionSpec as P

MESH = pl.DeviceIdType.MESH
ROWS = 16


def adamw(w, m, v, g):
    m = 0.9 * m + 0.1 * g
    v = 0.95 * v + 0.05 * g * g
    step = m * lax.rsqrt(v + 1e-8) + 0.1 * w
    return (w - 0.02 * step).astype(jnp.bfloat16), m, v


def kernel(n, layers, *refs):
    refs = iter(refs)
    take = lambda k: [next(refs) for _ in range(k)]
    g_hbm, w_hbm, m_hbm, v_hbm = take(3), take(3), take(3), take(3)
    w_out, m_out, v_out = take(3), take(3), take(3)
    terms, landed = take(3), take(3)
    load_sem, own_sem, rs_send, rs_recv, ag_send, ag_recv = refs

    me = lax.axis_index("dp")
    at = lambda k: lax.rem(me + (k + 2 * n), n)
    barrier = pltpu.get_barrier_semaphore()
    chunks = [(a, layer) for layer in range(layers) for a in range(3)]
    ways = (1, -1)
    far = n // 2

    def hops(c, way):
        return far if (c % 2 == 0) == (way == 1) else n - 1 - far

    def slot(c, way, s):
        return (0 if way == 1 else hops(c, 1)) + s - 1

    def new(a, layer, k):
        rows = w_out[a].shape[1] // n
        return w_out[a].at[layer, pl.ds(pl.multiple_of(at(k) * rows, ROWS), rows)]

    loads = {}

    def load(c, k):
        a, layer = chunks[c]
        loads[c, k % n] = pltpu.make_async_copy(g_hbm[a].at[layer, at(k)], terms[a].at[layer, at(k)], load_sem.at[c * n + k % n])
        loads[c, k % n].start()

    def loaded(c, k):
        loads[c, k % n].wait()

    for s in range(far):
        for c in range(len(chunks)):
            for way in ways:
                if hops(c, way) - s > 0:
                    load(c, way * (hops(c, way) - s))
    for c in range(len(chunks)):
        load(c, 0)
    own = {}
    for c, (a, layer) in enumerate(chunks):
        own[c] = [
            pltpu.make_async_copy(w_hbm[a].at[layer, me], new(a, layer, 0), own_sem.at[3 * c]),
            pltpu.make_async_copy(m_hbm[a].at[layer], m_out[a].at[layer], own_sem.at[3 * c + 1]),
            pltpu.make_async_copy(v_hbm[a].at[layer], v_out[a].at[layer], own_sem.at[3 * c + 2]),
        ]
        for copy in own[c]:
            copy.start()

    for way in ways:
        pl.semaphore_signal(barrier, inc=1, device_id={"dp": at(way)}, device_id_type=MESH)
    pl.semaphore_wait(barrier, 2)

    def sum_copy(c, way, s):
        a, layer = chunks[c]
        left = hops(c, way) - s + 1
        source = terms[a].at[layer, at(way * left)] if s == 1 else landed[a].at[layer, slot(c, way, s - 1)]
        i = c * (n - 1) + slot(c, way, s)
        return pltpu.make_async_remote_copy(
            src_ref=source,
            dst_ref=landed[a].at[layer, slot(c, way, s)],
            send_sem=rs_send.at[i],
            recv_sem=rs_recv.at[i],
            device_id={"dp": at(way)},
            device_id_type=MESH,
        )

    def new_copy(c, way, s):
        a, layer = chunks[c]
        block = new(a, layer, -way * (s - 1))
        i = c * (n - 1) + slot(c, way, s)
        return pltpu.make_async_remote_copy(
            src_ref=block,
            dst_ref=block,
            send_sem=ag_send.at[i],
            recv_sem=ag_recv.at[i],
            device_id={"dp": at(way)},
            device_id_type=MESH,
        )

    def arrived_new(c, way, s):
        a, layer = chunks[c]
        block = new(a, layer, -way * s)
        i = c * (n - 1) + slot(c, way, s)
        pltpu.make_async_remote_copy(
            src_ref=block,
            dst_ref=block,
            send_sem=ag_send.at[i],
            recv_sem=ag_recv.at[i],
            device_id={"dp": at(way)},
            device_id_type=MESH,
        ).wait_recv()

    def each(rows, body):
        def step(i, _):
            body(pl.ds(pl.multiple_of(i * ROWS, ROWS), ROWS))
            return 0

        lax.fori_loop(0, rows // ROWS, step, 0)

    def add(c, way, s):
        a, layer = chunks[c]
        sums, mine = landed[a].at[layer, slot(c, way, s)], terms[a].at[layer, at(way * (hops(c, way) - s))]

        def body(rows):
            sums[rows] = (sums[rows].astype(jnp.float32) + mine[rows].astype(jnp.float32)).astype(jnp.bfloat16)

        each(sums.shape[0], body)

    def update(c):
        a, layer = chunks[c]
        one = landed[a].at[layer, slot(c, 1, hops(c, 1))]
        two = landed[a].at[layer, slot(c, -1, hops(c, -1))]
        mine, w, m, v = terms[a].at[layer, me], new(a, layer, 0), m_out[a].at[layer], v_out[a].at[layer]

        def body(rows):
            g = one[rows].astype(jnp.float32) + two[rows].astype(jnp.float32) + mine[rows].astype(jnp.float32)
            g = g.astype(jnp.bfloat16).astype(jnp.float32)
            w[rows], m[rows], v[rows] = adamw(w[rows].astype(jnp.float32), m[rows], v[rows], g)

        each(one.shape[0], body)

    sent = []

    def start(copy):
        copy.start()
        sent.append(copy)

    everything = [(c, way) for c in range(len(chunks)) for way in ways]
    for c, way in everything:
        loaded(c, way * hops(c, way))
        start(sum_copy(c, way, 1))
    for s in range(1, far):
        for c, way in everything:
            if s < hops(c, way):
                sum_copy(c, way, s).wait_recv()
                loaded(c, way * (hops(c, way) - s))
                add(c, way, s)
                start(sum_copy(c, way, s + 1))
    for c in range(len(chunks)):
        for copy in own[c]:
            copy.wait()
        loaded(c, 0)
        for way in ways:
            sum_copy(c, way, hops(c, way)).wait_recv()
        update(c)
        for way in ways:
            start(new_copy(c, way, 1))
    for s in range(1, far + 1):
        for c, way in everything:
            if s <= hops(c, way):
                arrived_new(c, way, s)
                if s < hops(c, way):
                    start(new_copy(c, way, s + 1))
    for copy in sent:
        copy.wait_send()


def solution(mesh):
    n = mesh.shape["dp"]

    def step(*arrays):
        terms, weights, m, v = (arrays[i : i + 3] for i in (0, 3, 6, 9))
        layers = weights[0].shape[0]
        blocked = lambda w: w.reshape(layers, n, w.shape[-2] // n, w.shape[-1])
        whole = [jax.ShapeDtypeStruct(w.shape, w.dtype) for w in weights]
        terms, weights = [blocked(t[0]) for t in terms], [blocked(w) for w in weights]
        like = lambda x: pltpu.VMEM(x.shape, x.dtype)
        arrivals = layers * 3 * (n - 1)
        return pl.pallas_call(
            lambda *refs: kernel(n, layers, *refs),
            name="step",
            out_shape=[like(x) for x in (*whole, *m, *v)],
            in_specs=[pl.BlockSpec(memory_space=pltpu.HBM)] * 12,
            out_specs=[pl.BlockSpec(memory_space=pltpu.VMEM)] * 9,
            scratch_shapes=[
                *(pltpu.VMEM(w.shape, w.dtype) for w in weights),
                *(pltpu.VMEM((layers, n - 1, *w.shape[2:]), w.dtype) for w in weights),
                pltpu.SemaphoreType.DMA((layers * 3 * n,)),
                pltpu.SemaphoreType.DMA((layers * 3 * 3,)),
                *(pltpu.SemaphoreType.DMA((arrivals,)) for _ in range(4)),
            ],
            compiler_params=pltpu.CompilerParams(collective_id=0, has_side_effects=True, vmem_limit_bytes=40 << 20),
        )(*(pltpu.with_memory_space_constraint(x, pltpu.HBM) for x in (*terms, *weights, *m, *v)))

    all_of, cut = P(None, None, None), P(None, "dp", None)
    return jax.shard_map(
        step,
        mesh=mesh,
        in_specs=(P(("rep", "dp"), None, None, None),) * 3 + (all_of,) * 3 + (cut,) * 6,
        out_specs=(P("rep", None, None),) * 3 + (P("rep", "dp", None),) * 6,
        check_vma=False,
    )
```

time: 332 us -> 245 us (0.74)
  waiting for transfers between devices: 298 us -> 0 us
  Pallas kernels: 0 us -> 232 us
  between operations: 14.2 us -> 0.66 us
  other arithmetic: 8.94 us -> 0 us
    pallas_call x0 -> x1, Pallas kernels: none -> 232 us  [step(): pl.pallas_call(lambda *refs: kernel(n, layers, *refs), name='step', out_s...]
    reduce_scatter x3 -> x0, waiting for transfers between devices: 150 us -> none  [step(): lax.psum_scatter(t[0], 'dp', scatter_dimension=1, tiled=True)]
    all_gather x3 -> x0, waiting for transfers between devices: 146 us -> none  [step(): whole = [lax.all_gather(one[0], 'dp', axis=1, tiled=True) for one in new]]
    convert_element_type x3 -> x0, other arithmetic: 8.94 us -> none  [adamw(): return ((w - 0.02 * step).astype(jnp.bfloat16), m, v)]
    unnamed x17 -> x9, local copies, waits for them, and re-layouts: 9.93 us -> 11.4 us
  transfers between devices with their start and end apart: 6 -> 0, of which waited for: 6 -> 0; matrix products, arithmetic and copies ran while one was open for 3% -> 0% of each run, Pallas kernels for 0% -> 0%
where the time goes in v1:
time: 245 us
  Pallas kernels  232 us (95%)
  local copies, waits for them, and re-layouts  11.4 us (5%)
    pallas_call x1, Pallas kernels, step(): pl.pallas_call(lambda *refs: kernel(n, layers, *refs), name='step', out_s...  232 us
    unnamed x9, local copies, waits for them, and re-layouts  11.4 us

profile of v1, /device:TPU:22, one launch (start us, length us, event | category | flops | bytes accessed | tf_op | source)
XLA Modules:
  0.0 244.5 jit_solution(5854226912669381366)
XLA Ops:
  0.6 232.4 %step.1 = (bf16[2,640,1536]{2,1,0:T(8,128)(2,1)S(1)}, bf16[2,640,1536]{2,1,0:T(8,128)(2,1)S(1)}, bf16[2,1536,640]{2,1,0:T(8,128)(2,1)S(1)}, f32[2,80,1536]{2,1,0...) custom-call(bf16[2,8,80,1536]{3,2,1,0:T(8,128)(2,1)} %bitcast.6, ...), custom_call_target="tpu_custom_call" | custom-call | tf_op jit(solution)/shard_map/step/pallas_call | solution.py:191
  233.1 1.9 copy.30
  235.0 0.9 copy.33
  235.9 0.9 copy.34
  236.9 0.9 copy.35
  237.8 0.9 copy.36
  238.8 0.9 copy.37
  239.7 0.9 copy.38
  240.7 1.9 copy.31
  242.6 1.9 copy.32

commit v2 on v1

--- a/solution.py
+++ b/solution.py
@@ -177,6 +177,16 @@
         copy.wait_send()
 
 
+def put(*refs):
+    *refs, sem = refs
+    k = len(refs) // 2
+    copies = [pltpu.make_async_copy(a, b, sem.at[i]) for i, (a, b) in enumerate(zip(refs[:k], refs[k:], strict=True))]
+    for copy in copies:
+        copy.start()
+    for copy in copies:
+        copy.wait()
+
+
 def solution(mesh):
     n = mesh.shape["dp"]
 
@@ -188,7 +198,7 @@
         terms, weights = [blocked(t[0]) for t in terms], [blocked(w) for w in weights]
         like = lambda x: pltpu.VMEM(x.shape, x.dtype)
         arrivals = layers * 3 * (n - 1)
-        return pl.pallas_call(
+        out = pl.pallas_call(
             lambda *refs: kernel(n, layers, *refs),
             name="step",
             out_shape=[like(x) for x in (*whole, *m, *v)],
@@ -203,6 +213,15 @@
             ],
             compiler_params=pltpu.CompilerParams(collective_id=0, has_side_effects=True, vmem_limit_bytes=40 << 20),
         )(*(pltpu.with_memory_space_constraint(x, pltpu.HBM) for x in (*terms, *weights, *m, *v)))
+        return pl.pallas_call(
+            put,
+            name="put",
+            out_shape=[jax.ShapeDtypeStruct(x.shape, x.dtype) for x in out],
+            in_specs=[pl.BlockSpec(memory_space=pltpu.VMEM)] * 9,
+            out_specs=[pl.BlockSpec(memory_space=pl.ANY)] * 9,
+            scratch_shapes=[pltpu.SemaphoreType.DMA((9,))],
+            compiler_params=pltpu.CompilerParams(has_side_effects=True, vmem_limit_bytes=20 << 20),
+        )(*(pltpu.with_memory_space_constraint(x, pltpu.VMEM) for x in out))
 
     all_of, cut = P(None, None, None), P(None, "dp", None)
     return jax.shard_map(

time: 245 us -> 240 us (0.980)
  local copies, waits for them, and re-layouts: 11.4 us -> 0 us
  Pallas kernels: 232 us -> 239 us
    unnamed x9 -> x0, local copies, waits for them, and re-layouts: 11.4 us -> none
    pallas_call x0 -> x1, Pallas kernels: none -> 6.28 us  [step(): pl.pallas_call(put, name='put', out_shape=[jax.ShapeDtypeStruct(x.shape,...]
where the time goes in v2:
time: 240 us; the launch traced here: 239 us
  Pallas kernels  239 us (100%)
    pallas_call x1, Pallas kernels, step(): pl.pallas_call(lambda *refs: kernel(n, layers, *refs), name='step', out_s...  232 us
    pallas_call x1, Pallas kernels, step(): pl.pallas_call(put, name='put', out_shape=[jax.ShapeDtypeStruct(x.shape,...  6.28 us

profile of v2, /device:TPU:22, one launch (start us, length us, event | category | flops | bytes accessed | tf_op | source)
XLA Modules:
  0.0 239.3 jit_solution(7164161394044420208)
XLA Ops:
  0.6 232.4 %step.1 = (bf16[2,640,1536]{2,1,0:T(8,128)(2,1)S(1)}, bf16[2,640,1536]{2,1,0:T(8,128)(2,1)S(1)}, bf16[2,1536,640]{2,1,0:T(8,128)(2,1)S(1)}, f32[2,80,1536]{2,1,0...) custom-call(bf16[2,8,80,1536]{3,2,1,0:T(8,128)(2,1)} %bitcast.6, ...), custom_call_target="tpu_custom_call" | custom-call | tf_op jit(solution)/shard_map/step/pallas_call | solution.py:201
  233.1 6.3 %put.1 = (bf16[2,640,1536]{2,1,0:T(8,128)(2,1)}, bf16[2,640,1536]{2,1,0:T(8,128)(2,1)}, bf16[2,1536,640]{2,1,0:T(8,128)(2,1)}, f32[2,80,1536]{2,1,0:T(8,128)}, f...) custom-call(bf16[2,640,1536]{2,1,0:T(8,128)(2,1)S(1)} %get-tuple-ele, ...), custom_call_target="tpu_custom_call" | custom-call | tf_op jit(solution)/shard_map/put/pallas_call | solution.py:216

commit v3 on v2

v3 whole, which is shorter than its diff:
```python
import jax
import jax.numpy as jnp
from jax import lax
from jax.experimental import pallas as pl
from jax.experimental.pallas import tpu as pltpu
from jax.sharding import PartitionSpec as P

MESH = pl.DeviceIdType.MESH
ROWS = 16
LATE = 1
WAYS = (1, -1)


def adamw(w, m, v, g):
    m = 0.9 * m + 0.1 * g
    v = 0.95 * v + 0.05 * g * g
    step = m * lax.rsqrt(v + 1e-8) + 0.1 * w
    return (w - 0.02 * step).astype(jnp.bfloat16), m, v


class Ring:
    def __init__(self, n, layers):
        self.n, self.layers, self.far = n, layers, n // 2
        self.chunks = [(a, layer) for layer in range(layers) for a in range(3)]
        self.both = [(c, way) for c in range(len(self.chunks)) for way in WAYS]
        self.arrivals = len(self.chunks) * (n - 1)

    def at(self, k):
        return lax.rem(lax.axis_index("dp") + (k + 2 * self.n), self.n)

    def waits(self):
        return lax.rem(lax.axis_index("rep"), 2) == 1

    def hops(self, c, way):
        return self.far if (c % 2 == 0) == (way == 1) else self.n - 1 - self.far

    def slot(self, c, way, s):
        return (0 if way == 1 else self.hops(c, 1)) + s - 1

    def late(self, c, s):
        return s >= self.far - (c >= len(self.chunks) - LATE)

    def late_hops(self):
        return [(c, way, s) for c, way in self.both for s in range(1, self.hops(c, way) + 1) if self.late(c, s)]

    def new(self, ref, layer, k):
        rows = ref.shape[1] // self.n
        return ref.at[layer, pl.ds(pl.multiple_of(self.at(k) * rows, ROWS), rows)]

    def greet(self):
        barrier = pltpu.get_barrier_semaphore()
        for way in WAYS:
            pl.semaphore_signal(barrier, inc=1, device_id={"dp": self.at(way)}, device_id_type=MESH)
        pl.semaphore_wait(barrier, 2)

    def send(self, source, target, send_sem, recv_sem, way):
        return pltpu.make_async_remote_copy(
            src_ref=source, dst_ref=target, send_sem=send_sem, recv_sem=recv_sem, device_id={"dp": self.at(way)}, device_id_type=MESH
        )


def each(rows, body):
    def step(i, _):
        body(pl.ds(pl.multiple_of(i * ROWS, ROWS), ROWS))
        return 0

    lax.fori_loop(0, rows // ROWS, step, 0)


def kernel(ring, *refs):
    refs = iter(refs)
    take = lambda k: [next(refs) for _ in range(k)]
    g_hbm, w_hbm, m_hbm, v_hbm = take(3), take(3), take(3), take(3)
    w_out, m_out, v_out = take(3), take(3), take(3)
    terms, landed = take(3), take(3)
    load_sem, own_sem, rs_send, rs_recv, ag_send, ag_recv = refs
    n, far, chunks, at, hops, slot = ring.n, ring.far, ring.chunks, ring.at, ring.hops, ring.slot

    loads = {}

    def load(c, k):
        a, layer = chunks[c]
        loads[c, k % n] = pltpu.make_async_copy(g_hbm[a].at[layer, at(k)], terms[a].at[layer, at(k)], load_sem.at[c * n + k % n])
        loads[c, k % n].start()

    def loaded(c, k):
        loads[c, k % n].wait()

    for s in range(far):
        for c, way in ring.both:
            if hops(c, way) - s > 0:
                load(c, way * (hops(c, way) - s))
    for c in range(len(chunks)):
        load(c, 0)
    own = {}
    for c, (a, layer) in enumerate(chunks):
        own[c] = [
            pltpu.make_async_copy(w_hbm[a].at[layer, at(0)], ring.new(w_out[a], layer, 0), own_sem.at[3 * c]),
            pltpu.make_async_copy(m_hbm[a].at[layer], m_out[a].at[layer], own_sem.at[3 * c + 1]),
            pltpu.make_async_copy(v_hbm[a].at[layer], v_out[a].at[layer], own_sem.at[3 * c + 2]),
        ]
        for copy in own[c]:
            copy.start()

    ring.greet()

    def sum_copy(c, way, s):
        a, layer = chunks[c]
        left = hops(c, way) - s + 1
        source = terms[a].at[layer, at(way * left)] if s == 1 else landed[a].at[layer, slot(c, way, s - 1)]
        i = c * (n - 1) + slot(c, way, s)
        return ring.send(source, landed[a].at[layer, slot(c, way, s)], rs_send.at[i], rs_recv.at[i], way)

    def new_copy(c, way, s, k):
        a, layer = chunks[c]
        block = ring.new(w_out[a], layer, k)
        i = c * (n - 1) + slot(c, way, s)
        return ring.send(block, block, ag_send.at[i], ag_recv.at[i], way)

    def add(c, way, s):
        a, layer = chunks[c]
        sums, mine = landed[a].at[layer, slot(c, way, s)], terms[a].at[layer, at(way * (hops(c, way) - s))]

        def body(rows):
            sums[rows] = (sums[rows].astype(jnp.float32) + mine[rows].astype(jnp.float32)).astype(jnp.bfloat16)

        each(sums.shape[0], body)

    def update(c):
        a, layer = chunks[c]
        one = landed[a].at[layer, slot(c, 1, hops(c, 1))]
        two = landed[a].at[layer, slot(c, -1, hops(c, -1))]
        mine, w, m, v = terms[a].at[layer, at(0)], ring.new(w_out[a], layer, 0), m_out[a].at[layer], v_out[a].at[layer]

        def body(rows):
            g = one[rows].astype(jnp.float32) + two[rows].astype(jnp.float32) + mine[rows].astype(jnp.float32)
            g = g.astype(jnp.bfloat16).astype(jnp.float32)
            w[rows], m[rows], v[rows] = adamw(w[rows].astype(jnp.float32), m[rows], v[rows], g)

        each(one.shape[0], body)

    sent = []

    def start(copy):
        copy.start()
        sent.append(copy)

    for c, way in ring.both:
        loaded(c, way * hops(c, way))
        start(sum_copy(c, way, 1))
    for s in range(1, far):
        for c, way in ring.both:
            if s < hops(c, way):
                sum_copy(c, way, s).wait_recv()
                loaded(c, way * (hops(c, way) - s))
                add(c, way, s)
                start(sum_copy(c, way, s + 1))
    for c in range(len(chunks)):
        for copy in own[c]:
            copy.wait()
        loaded(c, 0)
        for way in WAYS:
            sum_copy(c, way, hops(c, way)).wait_recv()
        update(c)
        for way in WAYS:
            start(new_copy(c, way, 1, 0))

    def unless_late(late, body):
        if late:
            pl.when(jnp.logical_not(ring.waits()))(body)
        else:
            body()

    for s in range(1, far + 1):
        for c, way in ring.both:
            if s <= hops(c, way):
                unless_late(ring.late(c, s), new_copy(c, way, s, -way * s).wait_recv)
                if s < hops(c, way):
                    unless_late(ring.late(c, s + 1), new_copy(c, way, s + 1, -way * s).start)
    for copy in sent:
        copy.wait_send()
    for c, way in ring.both:
        for s in range(2, hops(c, way) + 1):
            unless_late(ring.late(c, s), new_copy(c, way, s, -way * (s - 1)).wait_send)


def place(ring, c, way, s):
    a, layer = ring.chunks[c]
    return (a, layer, 0) if s == ring.far else (a, layer, 1 if way == 1 else 2)


def last(ring, *refs):
    w, out = refs[:3], refs[3:6]
    send_sem, recv_sem = refs[6:]
    late = ring.late_hops()
    ring.greet()

    def copy(c, way, s):
        a, layer = ring.chunks[c]
        if ring.late(c, s - 1):
            b, *where = place(ring, c, way, s - 1)
            source = out[b].at[*where]
        else:
            source = ring.new(w[a], layer, -way * (s - 1))
        b, *where = place(ring, c, way, s)
        i = late.index((c, way, s))
        return ring.send(source, out[b].at[*where], send_sem.at[i], recv_sem.at[i], way)

    @pl.when(ring.waits())
    def _():
        first = [hop for hop in late if not ring.late(hop[0], hop[2] - 1)]
        then = [hop for hop in late if hop not in first]
        for hop in sorted(first, key=lambda hop: hop[2]):
            copy(*hop).start()
        for c, way, s in then:
            copy(c, way, s - 1).wait_recv()
            copy(c, way, s).start()
        for c, way, s in late:
            if not ((c, way, s + 1) in late):
                copy(c, way, s).wait_recv()
        for hop in late:
            copy(*hop).wait_send()


def put(*refs):
    *refs, sem = refs
    k = len(refs) // 2
    copies = [pltpu.make_async_copy(a, b, sem.at[i]) for i, (a, b) in enumerate(zip(refs[:k], refs[k:], strict=True))]
    for copy in copies:
        copy.start()
    for copy in copies:
        copy.wait()


def put_last(ring, *refs):
    blocks, _, whole, sem = refs[:3], refs[3:6], refs[6:9], refs[9]

    @pl.when(ring.waits())
    def _():
        copies = []
        for i, (c, way, s) in enumerate(ring.late_hops()):
            a, layer, which = place(ring, c, way, s)
            copies.append(pltpu.make_async_copy(blocks[a].at[layer, which], ring.new(whole[a], layer, -way * s), sem.at[i]))
        for copy in copies:
            copy.start()
        for copy in copies:
            copy.wait()


def solution(mesh):
    n = mesh.shape["dp"]

    def step(*arrays):
        terms, weights, m, v = (arrays[i : i + 3] for i in (0, 3, 6, 9))
        ring = Ring(n, weights[0].shape[0])
        blocked = lambda w: w.reshape(ring.layers, n, w.shape[-2] // n, w.shape[-1])
        vmem = lambda x: pltpu.VMEM(x.shape, x.dtype)
        hbm = lambda x: pltpu.HBM(x.shape, x.dtype)
        keep = lambda space, arrays: [pltpu.with_memory_space_constraint(x, space) for x in arrays]
        spec = lambda space, k: [pl.BlockSpec(memory_space=space)] * k
        blocks = [blocked(w) for w in weights]
        arrived = [jax.ShapeDtypeStruct((ring.layers, n - 1, *b.shape[2:]), b.dtype) for b in blocks]
        ends = [jax.ShapeDtypeStruct((ring.layers, 3, *b.shape[2:]), b.dtype) for b in blocks]
        late = len(ring.late_hops())

        out = pl.pallas_call(
            lambda *refs: kernel(ring, *refs),
            name="step",
            out_shape=[vmem(x) for x in (*weights, *m, *v)],
            in_specs=spec(pltpu.HBM, 12),
            out_specs=spec(pltpu.VMEM, 9),
            scratch_shapes=[
                *(pltpu.VMEM(x.shape, x.dtype) for x in (*blocks, *arrived)),
                pltpu.SemaphoreType.DMA((len(ring.chunks) * n,)),
                pltpu.SemaphoreType.DMA((len(ring.chunks) * 3,)),
                *(pltpu.SemaphoreType.DMA((ring.arrivals,)) for _ in range(4)),
            ],
            compiler_params=pltpu.CompilerParams(collective_id=0, has_side_effects=True, vmem_limit_bytes=40 << 20),
        )(*keep(pltpu.HBM, [blocked(t[0]) for t in terms] + blocks + [*m, *v]))
        stored = pl.pallas_call(
            put,
            name="put",
            out_shape=[hbm(x) for x in out],
            in_specs=spec(pltpu.VMEM, 9),
            out_specs=spec(pltpu.HBM, 9),
            scratch_shapes=[pltpu.SemaphoreType.DMA((9,))],
            compiler_params=pltpu.CompilerParams(has_side_effects=True, vmem_limit_bytes=20 << 20),
        )(*keep(pltpu.VMEM, out))
        rest = pl.pallas_call(
            lambda *refs: last(ring, *refs),
            name="last",
            out_shape=[vmem(x) for x in ends],
            in_specs=spec(pltpu.VMEM, 3),
            out_specs=spec(pltpu.VMEM, 3),
            scratch_shapes=[pltpu.SemaphoreType.DMA((late,)), pltpu.SemaphoreType.DMA((late,))],
            compiler_params=pltpu.CompilerParams(collective_id=1, has_side_effects=True, vmem_limit_bytes=20 << 20),
        )(*keep(pltpu.VMEM, out[:3]))
        whole = pl.pallas_call(
            lambda *refs: put_last(ring, *refs),
            name="put_last",
            out_shape=[hbm(w) for w in weights],
            in_specs=spec(pltpu.VMEM, 3) + spec(pltpu.HBM, 3),
            out_specs=spec(pltpu.HBM, 3),
            input_output_aliases={3: 0, 4: 1, 5: 2},
            scratch_shapes=[pltpu.SemaphoreType.DMA((late,))],
            compiler_params=pltpu.CompilerParams(has_side_effects=True, vmem_limit_bytes=20 << 20),
        )(*keep(pltpu.VMEM, rest), *keep(pltpu.HBM, stored[:3]))
        return (*whole, *stored[3:])

    all_of, cut = P(None, None, None), P(None, "dp", None)
    return jax.shard_map(
        step,
        mesh=mesh,
        in_specs=(P(("rep", "dp"), None, None, None),) * 3 + (all_of,) * 3 + (cut,) * 6,
        out_specs=(P("rep", None, None),) * 3 + (P("rep", "dp", None),) * 6,
        check_vma=False,
    )
```

time: 240 us -> 234 us (0.975)
  Pallas kernels: 239 us -> 231 us
    pallas_call x2 -> x4, Pallas kernels: 239 us -> 231 us  [the longest x1 222 us: step(): pl.pallas_call(lambda *refs: kernel(ring, *refs), name='step', out_shape=...]
where the time goes in v3:
time: 234 us; the launch traced here: 231 us
  Pallas kernels  231 us (99%)
    pallas_call x1, Pallas kernels, step(): pl.pallas_call(lambda *refs: kernel(ring, *refs), name='step', out_shape=...  222 us
    pallas_call x1, Pallas kernels, step(): pl.pallas_call(put, name='put', out_shape=[hbm(x) for x in out], in_specs...  6.28 us

profile of v3, /device:TPU:22, one launch (start us, length us, event | category | flops | bytes accessed | tf_op | source)
XLA Modules:
  0.0 231.3 jit_solution(9684728877361981907)
XLA Ops:
  0.6 221.9 %step.1 = (bf16[2,640,1536]{2,1,0:T(8,128)(2,1)S(1)}, bf16[2,640,1536]{2,1,0:T(8,128)(2,1)S(1)}, bf16[2,1536,640]{2,1,0:T(8,128)(2,1)S(1)}, f32[2,80,1536]{2,1,0...) custom-call(bf16[2,8,80,1536]{3,2,1,0:T(8,128)(2,1)} %bitcast.6, ...), custom_call_target="tpu_custom_call" | custom-call | tf_op jit(solution)/shard_map/step/pallas_call | solution.py:266
  222.5 6.3 %put.1 = (bf16[2,640,1536]{2,1,0:T(8,128)(2,1)}, bf16[2,640,1536]{2,1,0:T(8,128)(2,1)}, bf16[2,1536,640]{2,1,0:T(8,128)(2,1)}, f32[2,80,1536]{2,1,0:T(8,128)}, f...) custom-call(bf16[2,640,1536]{2,1,0:T(8,128)(2,1)S(1)} %get-tuple-ele, ...), custom_call_target="tpu_custom_call" | custom-call | tf_op jit(solution)/shard_map/put/pallas_call | solution.py:280
  228.8 2.4 %last.1 = (bf16[2,3,80,1536]{3,2,1,0:T(8,128)(2,1)S(1)}, bf16[2,3,80,1536]{3,2,1,0:T(8,128)(2,1)S(1)}, bf16[2,3,192,640]{3,2,1,0:T(8,128)(2,1)S(1)}) custom-call(bf16[2,640,1536]{2,1,0:T(8,128)(2,1)S(1)} %get-tuple-element.33.refs_0_, bf16[2,640,1536]{2,1,0:T(8,128)(2,1)S(1)} %get-tuple-element.34.refs_1_, bf16[2,1536,640]{2,1,0:T(8,128)(2,1)S(1)} %get-tuple-element.35.refs_2_), custom_call_target="tpu_custom_call" | custom-call | tf_op jit(solution)/shard_map/last/pallas_call | solution.py:289
  231.2 0.1 put_last.1

commit v4 on v3

v4 whole, which is shorter than its diff:
```python
import jax
import jax.numpy as jnp
from jax import lax
from jax.experimental import pallas as pl
from jax.experimental.pallas import tpu as pltpu
from jax.sharding import PartitionSpec as P

MESH = pl.DeviceIdType.MESH
ROWS = 16
LATE = 2
WAYS = (1, -1)


def adamw(w, m, v, g):
    m = 0.9 * m + 0.1 * g
    v = 0.95 * v + 0.05 * g * g
    step = m * lax.rsqrt(v + 1e-8) + 0.1 * w
    return (w - 0.02 * step).astype(jnp.bfloat16), m, v


class Ring:
    def __init__(self, n, layers):
        self.n, self.layers, self.far = n, layers, n // 2
        self.chunks = [(a, layer) for layer in range(layers) for a in range(3)]
        self.both = [(c, way) for c in range(len(self.chunks)) for way in WAYS]
        self.arrivals = len(self.chunks) * (n - 1)

    def at(self, k):
        return lax.rem(lax.axis_index("dp") + (k + 2 * self.n), self.n)

    def waits(self):
        return lax.rem(lax.axis_index("rep"), 2) == 0

    def hops(self, c, way):
        return self.far if (c % 2 == 0) == (way == 1) else self.n - 1 - self.far

    def slot(self, c, way, s):
        return (0 if way == 1 else self.hops(c, 1)) + s - 1

    def late(self, c, s):
        return s >= self.far - (c >= len(self.chunks) - LATE)

    def late_hops(self):
        return [(c, way, s) for c, way in self.both for s in range(1, self.hops(c, way) + 1) if self.late(c, s)]

    def span(self, ref, count):
        rows = ref.shape[1] // self.n
        if count <= self.n:
            return ref.at[0, pl.ds(0, count * rows)]
        assert count % 2 == 0 and count <= 2 * self.n
        return ref.at[pl.ds(0, 2), pl.ds(0, count // 2 * rows)]

    def done(self, ref, count, sem):
        part = self.span(ref, count)
        pltpu.make_async_copy(part, part, sem).wait()

    def new(self, ref, layer, k):
        rows = ref.shape[1] // self.n
        return ref.at[layer, pl.ds(pl.multiple_of(self.at(k) * rows, ROWS), rows)]

    def greet(self):
        for way in WAYS:
            pl.semaphore_signal(pltpu.get_barrier_semaphore(), inc=1, device_id={"dp": self.at(way)}, device_id_type=MESH)

    def greeted(self):
        pl.semaphore_wait(pltpu.get_barrier_semaphore(), 2)

    def send(self, source, target, send_sem, recv_sem, way):
        return pltpu.make_async_remote_copy(
            src_ref=source, dst_ref=target, send_sem=send_sem, recv_sem=recv_sem, device_id={"dp": self.at(way)}, device_id_type=MESH
        )


def each(rows, body):
    def step(i, _):
        body(pl.ds(pl.multiple_of(i * ROWS, ROWS), ROWS))
        return 0

    lax.fori_loop(0, rows // ROWS, step, 0)


def kernel(ring, *refs):
    refs = iter(refs)
    take = lambda k: [next(refs) for _ in range(k)]
    g_hbm, w_hbm, m_hbm, v_hbm = take(3), take(3), take(3), take(3)
    w_out, m_out, v_out = take(3), take(3), take(3)
    terms, landed = take(3), take(3)
    first_sem, load_sem, own_sem, rs_send, rs_recv, ag_send, ag_recv = refs
    n, far, chunks, at, hops, slot = ring.n, ring.far, ring.chunks, ring.at, ring.hops, ring.slot

    def load(c, k, sem):
        a, layer = chunks[c]
        return pltpu.make_async_copy(g_hbm[a].at[layer, at(k)], terms[a].at[layer, at(k)], sem)

    def first(i):
        c, way = ring.both[i]
        return load(c, way * hops(c, way), first_sem.at[i])

    def others(c):
        return [k for k in range(n) if k not in [way * hops(c, way) % n for way in WAYS]]

    def loaded(c):
        a, layer = chunks[c]
        some = pl.ds(0, len(others(c)))
        pltpu.make_async_copy(g_hbm[a].at[layer, some], terms[a].at[layer, some], load_sem.at[c]).wait()

    ring.greet()
    for i in range(len(ring.both)):
        first(i).start()

    def sum_copy(c, way, s):
        a, layer = chunks[c]
        left = hops(c, way) - s + 1
        source = terms[a].at[layer, at(way * left)] if s == 1 else landed[a].at[layer, slot(c, way, s - 1)]
        i = c * (n - 1) + slot(c, way, s)
        return ring.send(source, landed[a].at[layer, slot(c, way, s)], rs_send.at[a], rs_recv.at[i], way)

    def new_copy(c, way, s, k):
        a, layer = chunks[c]
        block = ring.new(w_out[a], layer, k)
        i = c * (n - 1) + slot(c, way, s)
        return ring.send(block, block, ag_send.at[2 * c + ring.late(c, s)], ag_recv.at[i], way)

    def add(c, way, s):
        a, layer = chunks[c]
        sums, mine = landed[a].at[layer, slot(c, way, s)], terms[a].at[layer, at(way * (hops(c, way) - s))]

        def body(rows):
            sums[rows] = (sums[rows].astype(jnp.float32) + mine[rows].astype(jnp.float32)).astype(jnp.bfloat16)

        each(sums.shape[0], body)

    def update(c):
        a, layer = chunks[c]
        one = landed[a].at[layer, slot(c, 1, hops(c, 1))]
        two = landed[a].at[layer, slot(c, -1, hops(c, -1))]
        mine, w, m, v = terms[a].at[layer, at(0)], ring.new(w_out[a], layer, 0), m_out[a].at[layer], v_out[a].at[layer]

        def body(rows):
            g = one[rows].astype(jnp.float32) + two[rows].astype(jnp.float32) + mine[rows].astype(jnp.float32)
            g = g.astype(jnp.bfloat16).astype(jnp.float32)
            w[rows], m[rows], v[rows] = adamw(w[rows].astype(jnp.float32), m[rows], v[rows], g)

        each(one.shape[0], body)

    ring.greeted()
    for i, (c, way) in enumerate(ring.both):
        first(i).wait()
        sum_copy(c, way, 1).start()
    for c, (a, layer) in enumerate(chunks):
        for k in others(c):
            load(c, k, load_sem.at[c]).start()
    for c, (a, layer) in enumerate(chunks):
        pltpu.make_async_copy(w_hbm[a].at[layer, at(0)], ring.new(w_out[a], layer, 0), own_sem.at[0]).start()
    for a in range(3):
        pltpu.make_async_copy(m_hbm[a], m_out[a], own_sem.at[1 + a]).start()
        pltpu.make_async_copy(v_hbm[a], v_out[a], own_sem.at[4 + a]).start()

    for s in range(1, far):
        for c, way in ring.both:
            if s == 1 and way == WAYS[0]:
                loaded(c)
            if s < hops(c, way):
                sum_copy(c, way, s).wait_recv()
                add(c, way, s)
                sum_copy(c, way, s + 1).start()
    ring.done(w_out[0], len(chunks), own_sem.at[0])
    for a in range(3):
        pltpu.make_async_copy(m_hbm[a], m_out[a], own_sem.at[1 + a]).wait()
        pltpu.make_async_copy(v_hbm[a], v_out[a], own_sem.at[4 + a]).wait()
    for c in range(len(chunks)):
        for way in WAYS:
            sum_copy(c, way, hops(c, way)).wait_recv()
        update(c)
        for way in WAYS:
            new_copy(c, way, 1, 0).start()

    def unless_late(late, body):
        if late:
            pl.when(jnp.logical_not(ring.waits()))(body)
        else:
            body()

    for s in range(1, far + 1):
        for c, way in ring.both:
            if s <= hops(c, way):
                unless_late(ring.late(c, s), new_copy(c, way, s, -way * s).wait_recv)
                if s < hops(c, way):
                    unless_late(ring.late(c, s + 1), new_copy(c, way, s + 1, -way * s).start)
    for a in range(3):
        pltpu.make_async_copy(landed[a], landed[a], rs_send.at[a]).wait()
    for c, (a, layer) in enumerate(chunks):
        for late in (False, True):
            count = sum(ring.late(c, s) == late for way in WAYS for s in range(1, hops(c, way) + 1))
            unless_late(late, lambda: ring.done(w_out[a], count, ag_send.at[2 * c + late]))


def place(ring, c, way, s):
    a, layer = ring.chunks[c]
    return (a, layer, 0) if s == ring.far else (a, layer, 1 if way == 1 else 2)


def last(ring, *refs):
    w, out = refs[:3], refs[3:6]
    send_sem, recv_sem = refs[6:]
    late = ring.late_hops()
    first = [hop for hop in late if not ring.late(hop[0], hop[2] - 1)]
    then = [hop for hop in late if hop not in first]
    ring.greet()
    ring.greeted()

    def copy(c, way, s):
        a, layer = ring.chunks[c]
        if ring.late(c, s - 1):
            b, *where = place(ring, c, way, s - 1)
            source = out[b].at[*where]
        else:
            source = ring.new(w[a], layer, -way * (s - 1))
        b, *where = place(ring, c, way, s)
        i = then.index((c, way, s + 1)) if (c, way, s + 1) in then else len(then) + WAYS.index(way)
        return ring.send(source, out[b].at[*where], send_sem.at[0], recv_sem.at[i], way)

    @pl.when(ring.waits())
    def _():
        for hop in sorted(first, key=lambda hop: hop[2]):
            copy(*hop).start()
        for c, way, s in then:
            copy(c, way, s - 1).wait_recv()
            copy(c, way, s).start()
        for i, way in enumerate(WAYS):
            ends = [hop for hop in late if hop[1] == way and (*hop[:2], hop[2] + 1) not in then]
            ring.done(w[0], len(ends), recv_sem.at[len(then) + i])
        ring.done(w[0], len(late), send_sem.at[0])


def put(ring, *refs):
    here, there, sem = refs[:9], refs[9:18], refs[18]
    late = {(c, -way * s % ring.n) for c, way, s in ring.late_hops()}

    def whole(i):
        return pltpu.make_async_copy(here[i], there[i], sem.at[i])

    for i in range(3, 9):
        whole(i).start()

    @pl.when(jnp.logical_not(ring.waits()))
    def _():
        for i in range(3):
            whole(i).start()
        for i in range(3):
            whole(i).wait()

    @pl.when(ring.waits())
    def _():
        blocks = [(c, k) for c in range(len(ring.chunks)) for k in range(ring.n) if (c, k) not in late]
        for c, k in blocks:
            a, layer = ring.chunks[c]
            pltpu.make_async_copy(ring.new(here[a], layer, k), ring.new(there[a], layer, k), sem.at[9 + c]).start()
        for c, (a, layer) in enumerate(ring.chunks):
            count = sum(c == other for other, _ in blocks)
            pltpu.make_async_copy(ring.span(here[a], count), ring.span(there[a], count), sem.at[9 + c]).wait()

    for i in range(3, 9):
        whole(i).wait()


def put_last(ring, *refs):
    blocks, _, whole, sem = refs[:3], refs[3:6], refs[6:9], refs[9]

    @pl.when(ring.waits())
    def _():
        for c, way, s in ring.late_hops():
            a, layer, which = place(ring, c, way, s)
            pltpu.make_async_copy(blocks[a].at[layer, which], ring.new(whole[a], layer, -way * s), sem.at[0]).start()
        ring.done(whole[0], len(ring.late_hops()), sem.at[0])


def solution(mesh):
    n = mesh.shape["dp"]

    def step(*arrays):
        terms, weights, m, v = (arrays[i : i + 3] for i in (0, 3, 6, 9))
        ring = Ring(n, weights[0].shape[0])
        blocked = lambda w: w.reshape(ring.layers, n, w.shape[-2] // n, w.shape[-1])
        vmem = lambda x: pltpu.VMEM(x.shape, x.dtype)
        hbm = lambda x: pltpu.HBM(x.shape, x.dtype)
        keep = lambda space, arrays: [pltpu.with_memory_space_constraint(x, space) for x in arrays]
        spec = lambda space, k: [pl.BlockSpec(memory_space=space)] * k
        blocks = [blocked(w) for w in weights]
        arrived = [jax.ShapeDtypeStruct((ring.layers, n - 1, *b.shape[2:]), b.dtype) for b in blocks]
        ends = [jax.ShapeDtypeStruct((ring.layers, 3, *b.shape[2:]), b.dtype) for b in blocks]
        assert len({b.size for b in blocks}) == 1

        out = pl.pallas_call(
            lambda *refs: kernel(ring, *refs),
            name="step",
            out_shape=[vmem(x) for x in (*weights, *m, *v)],
            in_specs=spec(pltpu.HBM, 12),
            out_specs=spec(pltpu.VMEM, 9),
            scratch_shapes=[
                *(pltpu.VMEM(x.shape, x.dtype) for x in (*blocks, *arrived)),
                *(pltpu.SemaphoreType.DMA((k,)) for k in (2 * len(ring.chunks), len(ring.chunks), 7)),
                *(pltpu.SemaphoreType.DMA((k,)) for k in (3, ring.arrivals, 2 * len(ring.chunks), ring.arrivals)),
            ],
            compiler_params=pltpu.CompilerParams(collective_id=0, has_side_effects=True, vmem_limit_bytes=40 << 20),
        )(*keep(pltpu.HBM, [blocked(t[0]) for t in terms] + blocks + [*m, *v]))
        stored = pl.pallas_call(
            lambda *refs: put(ring, *refs),
            name="put",
            out_shape=[hbm(x) for x in out],
            in_specs=spec(pltpu.VMEM, 9),
            out_specs=spec(pltpu.HBM, 9),
            scratch_shapes=[pltpu.SemaphoreType.DMA((9 + len(ring.chunks),))],
            compiler_params=pltpu.CompilerParams(has_side_effects=True, vmem_limit_bytes=20 << 20),
        )(*keep(pltpu.VMEM, out))
        rest = pl.pallas_call(
            lambda *refs: last(ring, *refs),
            name="last",
            out_shape=[vmem(x) for x in ends],
            in_specs=spec(pltpu.VMEM, 3),
            out_specs=spec(pltpu.VMEM, 3),
            scratch_shapes=[pltpu.SemaphoreType.DMA((1,)), pltpu.SemaphoreType.DMA((LATE + 2,))],
            compiler_params=pltpu.CompilerParams(collective_id=1, has_side_effects=True, vmem_limit_bytes=20 << 20),
        )(*keep(pltpu.VMEM, out[:3]))
        whole = pl.pallas_call(
            lambda *refs: put_last(ring, *refs),
            name="put_last",
            out_shape=[hbm(w) for w in weights],
            in_specs=spec(pltpu.VMEM, 3) + spec(pltpu.HBM, 3),
            out_specs=spec(pltpu.HBM, 3),
            input_output_aliases={3: 0, 4: 1, 5: 2},
            scratch_shapes=[pltpu.SemaphoreType.DMA((1,))],
            compiler_params=pltpu.CompilerParams(has_side_effects=True, vmem_limit_bytes=20 << 20),
        )(*keep(pltpu.VMEM, rest), *keep(pltpu.HBM, stored[:3]))
        return (*whole, *stored[3:])

    all_of, cut = P(None, None, None), P(None, "dp", None)
    return jax.shard_map(
        step,
        mesh=mesh,
        in_specs=(P(("rep", "dp"), None, None, None),) * 3 + (all_of,) * 3 + (cut,) * 6,
        out_specs=(P("rep", None, None),) * 3 + (P("rep", "dp", None),) * 6,
        check_vma=False,
    )
```

time: 234 us -> 233 us (level)
    pallas_call x1, Pallas kernels: 2.4 us -> 19 us  [step(): pl.pallas_call(lambda *refs: last(ring, *refs), name='last', out_shape=[v...]
    pallas_call x1, Pallas kernels: 222 us -> 206 us  [step(): pl.pallas_call(lambda *refs: kernel(ring, *refs), name='step', out_shape=...]
where the time goes in v4:
time: 233 us; the launch traced here: 232 us
  Pallas kernels  232 us (100%)
    pallas_call x1, Pallas kernels, step(): pl.pallas_call(lambda *refs: kernel(ring, *refs), name='step', out_shape=...  206 us
    pallas_call x1, Pallas kernels, step(): pl.pallas_call(lambda *refs: last(ring, *refs), name='last', out_shape=[v...  19 us
    pallas_call x1, Pallas kernels, step(): pl.pallas_call(lambda *refs: put(ring, *refs), name='put', out_shape=[hbm...  5.48 us

profile of v4, /device:TPU:22, one launch (start us, length us, event | category | flops | bytes accessed | tf_op | source)
XLA Modules:
  0.0 232.4 jit_solution(18060493141144879976)
XLA Ops:
  0.6 205.8 %step.1 = (bf16[2,640,1536]{2,1,0:T(8,128)(2,1)S(1)}, bf16[2,640,1536]{2,1,0:T(8,128)(2,1)S(1)}, bf16[2,1536,640]{2,1,0:T(8,128)(2,1)S(1)}, f32[2,80,1536]{2,1,0...) custom-call(bf16[2,8,80,1536]{3,2,1,0:T(8,128)(2,1)} %bitcast.6, ...), custom_call_target="tpu_custom_call" | custom-call | tf_op jit(solution)/shard_map/step/pallas_call | solution.py:294
  206.5 5.5 %put.1 = (bf16[2,640,1536]{2,1,0:T(8,128)(2,1)}, bf16[2,640,1536]{2,1,0:T(8,128)(2,1)}, bf16[2,1536,640]{2,1,0:T(8,128)(2,1)}, f32[2,80,1536]{2,1,0:T(8,128)}, f...) custom-call(bf16[2,640,1536]{2,1,0:T(8,128)(2,1)S(1)} %get-tuple-ele, ...), custom_call_target="tpu_custom_call" | custom-call | tf_op jit(solution)/shard_map/put/pallas_call | solution.py:307
  212.0 19.0 %last.1 = (bf16[2,3,80,1536]{3,2,1,0:T(8,128)(2,1)S(1)}, bf16[2,3,80,1536]{3,2,1,0:T(8,128)(2,1)S(1)}, bf16[2,3,192,640]{3,2,1,0:T(8,128)(2,1)S(1)}) custom-call(bf16[2,640,1536]{2,1,0:T(8,128)(2,1)S(1)} %get-tuple-element.33.refs_0_, bf16[2,640,1536]{2,1,0:T(8,128)(2,1)S(1)} %get-tuple-element.34.refs_1_, bf16[2,1536,640]{2,1,0:T(8,128)(2,1)S(1)} %get-tuple-element.35.refs_2_), custom_call_target="tpu_custom_call" | custom-call | tf_op jit(solution)/shard_map/last/pallas_call | solution.py:316
  231.0 1.4 put_last.1

commit v5 on v4

--- a/solution.py
+++ b/solution.py
@@ -23,7 +23,6 @@
         self.n, self.layers, self.far = n, layers, n // 2
         self.chunks = [(a, layer) for layer in range(layers) for a in range(3)]
         self.both = [(c, way) for c in range(len(self.chunks)) for way in WAYS]
-        self.arrivals = len(self.chunks) * (n - 1)
 
     def at(self, k):
         return lax.rem(lax.axis_index("dp") + (k + 2 * self.n), self.n)
@@ -112,14 +111,17 @@
         a, layer = chunks[c]
         left = hops(c, way) - s + 1
         source = terms[a].at[layer, at(way * left)] if s == 1 else landed[a].at[layer, slot(c, way, s - 1)]
-        i = c * (n - 1) + slot(c, way, s)
-        return ring.send(source, landed[a].at[layer, slot(c, way, s)], rs_send.at[a], rs_recv.at[i], way)
+        return ring.send(source, landed[a].at[layer, slot(c, way, s)], rs_send.at[a], rs_recv.at[c * far + s - 1], way)
+
+    def sums_arrived(c, s):
+        a, layer = chunks[c]
+        some = landed[a].at[layer, pl.ds(0, sum(s <= hops(c, way) for way in WAYS))]
+        pltpu.make_async_copy(some, some, rs_recv.at[c * far + s - 1]).wait()
 
     def new_copy(c, way, s, k):
         a, layer = chunks[c]
         block = ring.new(w_out[a], layer, k)
-        i = c * (n - 1) + slot(c, way, s)
-        return ring.send(block, block, ag_send.at[2 * c + ring.late(c, s)], ag_recv.at[i], way)
+        return ring.send(block, block, ag_send.at[2 * c + ring.late(c, s)], ag_recv.at[c * far + s - 1], way)
 
     def add(c, way, s):
         a, layer = chunks[c]
@@ -157,20 +159,20 @@
         pltpu.make_async_copy(v_hbm[a], v_out[a], own_sem.at[4 + a]).start()
 
     for s in range(1, far):
-        for c, way in ring.both:
-            if s == 1 and way == WAYS[0]:
+        for c in range(len(chunks)):
+            if s == 1:
                 loaded(c)
-            if s < hops(c, way):
-                sum_copy(c, way, s).wait_recv()
-                add(c, way, s)
-                sum_copy(c, way, s + 1).start()
+            sums_arrived(c, s)
+            for way in WAYS:
+                if s < hops(c, way):
+                    add(c, way, s)
+                    sum_copy(c, way, s + 1).start()
     ring.done(w_out[0], len(chunks), own_sem.at[0])
     for a in range(3):
         pltpu.make_async_copy(m_hbm[a], m_out[a], own_sem.at[1 + a]).wait()
         pltpu.make_async_copy(v_hbm[a], v_out[a], own_sem.at[4 + a]).wait()
     for c in range(len(chunks)):
-        for way in WAYS:
-            sum_copy(c, way, hops(c, way)).wait_recv()
+        sums_arrived(c, far)
         update(c)
         for way in WAYS:
             new_copy(c, way, 1, 0).start()
@@ -182,9 +184,10 @@
             body()
 
     for s in range(1, far + 1):
-        for c, way in ring.both:
-            if s <= hops(c, way):
-                unless_late(ring.late(c, s), new_copy(c, way, s, -way * s).wait_recv)
+        for c, (a, layer) in enumerate(chunks):
+            count = sum(s <= hops(c, way) for way in WAYS)
+            unless_late(ring.late(c, s), lambda: ring.done(w_out[a], count, ag_recv.at[c * far + s - 1]))
+            for way in WAYS:
                 if s < hops(c, way):
                     unless_late(ring.late(c, s + 1), new_copy(c, way, s + 1, -way * s).start)
     for a in range(3):
@@ -204,8 +207,9 @@
     w, out = refs[:3], refs[3:6]
     send_sem, recv_sem = refs[6:]
     late = ring.late_hops()
-    first = [hop for hop in late if not ring.late(hop[0], hop[2] - 1)]
-    then = [hop for hop in late if hop not in first]
+    shared = [(c, way, ring.far) for c, way in ring.both if c == 0]
+    first = [hop for hop in late if not ring.late(hop[0], hop[2] - 1) and hop not in shared]
+    then = [hop for hop in late if ring.late(hop[0], hop[2] - 1)]
     ring.greet()
     ring.greeted()
 
@@ -217,20 +221,31 @@
         else:
             source = ring.new(w[a], layer, -way * (s - 1))
         b, *where = place(ring, c, way, s)
-        i = then.index((c, way, s + 1)) if (c, way, s + 1) in then else len(then) + WAYS.index(way)
-        return ring.send(source, out[b].at[*where], send_sem.at[0], recv_sem.at[i], way)
+        if (c, way, s) in shared:
+            i = shared.index((c, way, s))
+            side = source.shape[0] // ROWS * 2 // 5 * ROWS
+            rows = pl.ds(0, source.shape[0] - side) if (c, way, s) in late else pl.ds(source.shape[0] - side, side)
+            return ring.send(source.at[rows], out[b].at[*where, rows], send_sem.at[2 + i], recv_sem.at[i], way)
+        if (c, way, s + 1) in then:
+            i = 4 + then.index((c, way, s + 1))
+        else:
+            i = 2 + WAYS.index(way)
+        return ring.send(source, out[b].at[*where], send_sem.at[int((c, way, s) in then)], recv_sem.at[i], way)
 
     @pl.when(ring.waits())
     def _():
-        for hop in sorted(first, key=lambda hop: hop[2]):
+        for hop in sorted(first + shared, key=lambda hop: (hop[2], hop[0])):
             copy(*hop).start()
         for c, way, s in then:
             copy(c, way, s - 1).wait_recv()
             copy(c, way, s).start()
         for i, way in enumerate(WAYS):
-            ends = [hop for hop in late if hop[1] == way and (*hop[:2], hop[2] + 1) not in then]
-            ring.done(w[0], len(ends), recv_sem.at[len(then) + i])
-        ring.done(w[0], len(late), send_sem.at[0])
+            ends = [hop for hop in first + then if hop[1] == way and (*hop[:2], hop[2] + 1) not in then]
+            ring.done(w[0], len(ends), recv_sem.at[2 + i])
+        ring.done(w[0], len(first), send_sem.at[0])
+        ring.done(w[0], len(then), send_sem.at[1])
+        for hop in shared:
+            copy(*hop).wait()
 
 
 def put(ring, *refs):
@@ -300,7 +315,7 @@
             scratch_shapes=[
                 *(pltpu.VMEM(x.shape, x.dtype) for x in (*blocks, *arrived)),
                 *(pltpu.SemaphoreType.DMA((k,)) for k in (2 * len(ring.chunks), len(ring.chunks), 7)),
-                *(pltpu.SemaphoreType.DMA((k,)) for k in (3, ring.arrivals, 2 * len(ring.chunks), ring.arrivals)),
+                *(pltpu.SemaphoreType.DMA((k,)) for k in (3, len(ring.chunks) * ring.far, 2 * len(ring.chunks), len(ring.chunks) * ring.far)),
             ],
             compiler_params=pltpu.CompilerParams(collective_id=0, has_side_effects=True, vmem_limit_bytes=40 << 20),
         )(*keep(pltpu.HBM, [blocked(t[0]) for t in terms] + blocks + [*m, *v]))
@@ -319,7 +334,7 @@
             out_shape=[vmem(x) for x in ends],
             in_specs=spec(pltpu.VMEM, 3),
             out_specs=spec(pltpu.VMEM, 3),
-            scratch_shapes=[pltpu.SemaphoreType.DMA((1,)), pltpu.SemaphoreType.DMA((LATE + 2,))],
+            scratch_shapes=[pltpu.SemaphoreType.DMA((4,)), pltpu.SemaphoreType.DMA((LATE + 4,))],
             compiler_params=pltpu.CompilerParams(collective_id=1, has_side_effects=True, vmem_limit_bytes=20 << 20),
         )(*keep(pltpu.VMEM, out[:3]))
         whole = pl.pallas_call(

time: 233 us -> 232 us (level)
  no operation moved by 1% of the time
where the time goes in v5:
time: 232 us
  Pallas kernels  231 us (100%)
    pallas_call x1, Pallas kernels, step(): pl.pallas_call(lambda *refs: kernel(ring, *refs), name='step', out_shape=...  206 us
    pallas_call x1, Pallas kernels, step(): pl.pallas_call(lambda *refs: last(ring, *refs), name='last', out_shape=[v...  18.7 us
    pallas_call x1, Pallas kernels, step(): pl.pallas_call(lambda *refs: put(ring, *refs), name='put', out_shape=[hbm...  5.48 us

profile of v5, /device:TPU:22, one launch (start us, length us, event | category | flops | bytes accessed | tf_op | source)
XLA Modules:
  0.0 231.8 jit_solution(16623535705012392099)
XLA Ops:
  0.6 205.5 %step.1 = (bf16[2,640,1536]{2,1,0:T(8,128)(2,1)S(1)}, bf16[2,640,1536]{2,1,0:T(8,128)(2,1)S(1)}, bf16[2,1536,640]{2,1,0:T(8,128)(2,1)S(1)}, f32[2,80,1536]{2,1,0...) custom-call(bf16[2,8,80,1536]{3,2,1,0:T(8,128)(2,1)} %bitcast.6, ...), custom_call_target="tpu_custom_call" | custom-call | tf_op jit(solution)/shard_map/step/pallas_call | solution.py:309
  206.2 5.5 %put.1 = (bf16[2,640,1536]{2,1,0:T(8,128)(2,1)}, bf16[2,640,1536]{2,1,0:T(8,128)(2,1)}, bf16[2,1536,640]{2,1,0:T(8,128)(2,1)}, f32[2,80,1536]{2,1,0:T(8,128)}, f...) custom-call(bf16[2,640,1536]{2,1,0:T(8,128)(2,1)S(1)} %get-tuple-ele, ...), custom_call_target="tpu_custom_call" | custom-call | tf_op jit(solution)/shard_map/put/pallas_call | solution.py:322
  211.7 18.7 %last.1 = (bf16[2,3,80,1536]{3,2,1,0:T(8,128)(2,1)S(1)}, bf16[2,3,80,1536]{3,2,1,0:T(8,128)(2,1)S(1)}, bf16[2,3,192,640]{3,2,1,0:T(8,128)(2,1)S(1)}) custom-call(bf16[2,640,1536]{2,1,0:T(8,128)(2,1)S(1)} %get-tuple-element.33.refs_0_, bf16[2,640,1536]{2,1,0:T(8,128)(2,1)S(1)} %get-tuple-element.34.refs_1_, bf16[2,1536,640]{2,1,0:T(8,128)(2,1)S(1)} %get-tuple-element.35.refs_2_), custom_call_target="tpu_custom_call" | custom-call | tf_op jit(solution)/shard_map/last/pallas_call | solution.py:331
  230.3 1.4 put_last.1

commit v6 on v5

--- a/solution.py
+++ b/solution.py
@@ -223,7 +223,7 @@
         b, *where = place(ring, c, way, s)
         if (c, way, s) in shared:
             i = shared.index((c, way, s))
-            side = source.shape[0] // ROWS * 2 // 5 * ROWS
+            side = source.shape[0] * 3 // 10 // 8 * 8
             rows = pl.ds(0, source.shape[0] - side) if (c, way, s) in late else pl.ds(source.shape[0] - side, side)
             return ring.send(source.at[rows], out[b].at[*where, rows], send_sem.at[2 + i], recv_sem.at[i], way)
         if (c, way, s + 1) in then:
@@ -234,11 +234,13 @@
 
     @pl.when(ring.waits())
     def _():
-        for hop in sorted(first + shared, key=lambda hop: (hop[2], hop[0])):
+        for hop in sorted(first, key=lambda hop: (hop[2], hop[0])):
             copy(*hop).start()
         for c, way, s in then:
             copy(c, way, s - 1).wait_recv()
             copy(c, way, s).start()
+        for hop in shared:
+            copy(*hop).start()
         for i, way in enumerate(WAYS):
             ends = [hop for hop in first + then if hop[1] == way and (*hop[:2], hop[2] + 1) not in then]
             ring.done(w[0], len(ends), recv_sem.at[2 + i])

time: 232 us -> 232 us (level)
  no operation moved by 1% of the time
where the time goes in v6:
time: 232 us
  Pallas kernels  231 us (100%)
    pallas_call x1, Pallas kernels, step(): pl.pallas_call(lambda *refs: kernel(ring, *refs), name='step', out_shape=...  206 us
    pallas_call x1, Pallas kernels, step(): pl.pallas_call(lambda *refs: last(ring, *refs), name='last', out_shape=[v...  18.6 us
    pallas_call x1, Pallas kernels, step(): pl.pallas_call(lambda *refs: put(ring, *refs), name='put', out_shape=[hbm...  5.48 us

profile of v6, /device:TPU:22, one launch (start us, length us, event | category | flops | bytes accessed | tf_op | source)
XLA Modules:
  0.0 231.7 jit_solution(14494085519674077579)
XLA Ops:
  0.6 205.5 %step.1 = (bf16[2,640,1536]{2,1,0:T(8,128)(2,1)S(1)}, bf16[2,640,1536]{2,1,0:T(8,128)(2,1)S(1)}, bf16[2,1536,640]{2,1,0:T(8,128)(2,1)S(1)}, f32[2,80,1536]{2,1,0...) custom-call(bf16[2,8,80,1536]{3,2,1,0:T(8,128)(2,1)} %bitcast.6, ...), custom_call_target="tpu_custom_call" | custom-call | tf_op jit(solution)/shard_map/step/pallas_call | solution.py:311
  206.2 5.5 %put.1 = (bf16[2,640,1536]{2,1,0:T(8,128)(2,1)}, bf16[2,640,1536]{2,1,0:T(8,128)(2,1)}, bf16[2,1536,640]{2,1,0:T(8,128)(2,1)}, f32[2,80,1536]{2,1,0:T(8,128)}, f...) custom-call(bf16[2,640,1536]{2,1,0:T(8,128)(2,1)S(1)} %get-tuple-ele, ...), custom_call_target="tpu_custom_call" | custom-call | tf_op jit(solution)/shard_map/put/pallas_call | solution.py:324
  211.7 18.6 %last.1 = (bf16[2,3,80,1536]{3,2,1,0:T(8,128)(2,1)S(1)}, bf16[2,3,80,1536]{3,2,1,0:T(8,128)(2,1)S(1)}, bf16[2,3,192,640]{3,2,1,0:T(8,128)(2,1)S(1)}) custom-call(bf16[2,640,1536]{2,1,0:T(8,128)(2,1)S(1)} %get-tuple-element.33.refs_0_, bf16[2,640,1536]{2,1,0:T(8,128)(2,1)S(1)} %get-tuple-element.34.refs_1_, bf16[2,1536,640]{2,1,0:T(8,128)(2,1)S(1)} %get-tuple-element.35.refs_2_), custom_call_target="tpu_custom_call" | custom-call | tf_op jit(solution)/shard_map/last/pallas_call | solution.py:333
  230.2 1.4 put_last.1

commit v7 on v6

--- a/solution.py
+++ b/solution.py
@@ -84,16 +84,12 @@
     g_hbm, w_hbm, m_hbm, v_hbm = take(3), take(3), take(3), take(3)
     w_out, m_out, v_out = take(3), take(3), take(3)
     terms, landed = take(3), take(3)
-    first_sem, load_sem, own_sem, rs_send, rs_recv, ag_send, ag_recv = refs
+    load_sem, own_sem, rs_send, rs_recv, ag_send, ag_recv = refs
     n, far, chunks, at, hops, slot = ring.n, ring.far, ring.chunks, ring.at, ring.hops, ring.slot
 
     def load(c, k, sem):
         a, layer = chunks[c]
         return pltpu.make_async_copy(g_hbm[a].at[layer, at(k)], terms[a].at[layer, at(k)], sem)
-
-    def first(i):
-        c, way = ring.both[i]
-        return load(c, way * hops(c, way), first_sem.at[i])
 
     def others(c):
         return [k for k in range(n) if k not in [way * hops(c, way) % n for way in WAYS]]
@@ -104,13 +100,11 @@
         pltpu.make_async_copy(g_hbm[a].at[layer, some], terms[a].at[layer, some], load_sem.at[c]).wait()
 
     ring.greet()
-    for i in range(len(ring.both)):
-        first(i).start()
 
     def sum_copy(c, way, s):
         a, layer = chunks[c]
         left = hops(c, way) - s + 1
-        source = terms[a].at[layer, at(way * left)] if s == 1 else landed[a].at[layer, slot(c, way, s - 1)]
+        source = g_hbm[a].at[layer, at(way * left)] if s == 1 else landed[a].at[layer, slot(c, way, s - 1)]
         return ring.send(source, landed[a].at[layer, slot(c, way, s)], rs_send.at[a], rs_recv.at[c * far + s - 1], way)
 
     def sums_arrived(c, s):
@@ -146,8 +140,7 @@
         each(one.shape[0], body)
 
     ring.greeted()
-    for i, (c, way) in enumerate(ring.both):
-        first(i).wait()
+    for c, way in ring.both:
         sum_copy(c, way, 1).start()
     for c, (a, layer) in enumerate(chunks):
         for k in others(c):
@@ -316,7 +309,7 @@
             out_specs=spec(pltpu.VMEM, 9),
             scratch_shapes=[
                 *(pltpu.VMEM(x.shape, x.dtype) for x in (*blocks, *arrived)),
-                *(pltpu.SemaphoreType.DMA((k,)) for k in (2 * len(ring.chunks), len(ring.chunks), 7)),
+                *(pltpu.SemaphoreType.DMA((k,)) for k in (len(ring.chunks), 7)),
                 *(pltpu.SemaphoreType.DMA((k,)) for k in (3, len(ring.chunks) * ring.far, 2 * len(ring.chunks), len(ring.chunks) * ring.far)),
             ],
             compiler_params=pltpu.CompilerParams(collective_id=0, has_side_effects=True, vmem_limit_bytes=40 << 20),

time: 232 us -> 232 us (level)
  no operation moved by 1% of the time
where the time goes in v7:
time: 232 us
  Pallas kernels  231 us (100%)
    pallas_call x1, Pallas kernels, step(): pl.pallas_call(lambda *refs: kernel(ring, *refs), name='step', out_shape=...  205 us
    pallas_call x1, Pallas kernels, step(): pl.pallas_call(lambda *refs: last(ring, *refs), name='last', out_shape=[v...  18.7 us
    pallas_call x1, Pallas kernels, step(): pl.pallas_call(lambda *refs: put(ring, *refs), name='put', out_shape=[hbm...  5.48 us

profile of v7, /device:TPU:22, one launch (start us, length us, event | category | flops | bytes accessed | tf_op | source)
XLA Modules:
  0.0 231.5 jit_solution(8754862041134574772)
XLA Ops:
  0.6 205.2 %step.1 = (bf16[2,640,1536]{2,1,0:T(8,128)(2,1)S(1)}, bf16[2,640,1536]{2,1,0:T(8,128)(2,1)S(1)}, bf16[2,1536,640]{2,1,0:T(8,128)(2,1)S(1)}, f32[2,80,1536]{2,1,0...) custom-call(bf16[2,8,80,1536]{3,2,1,0:T(8,128)(2,1)} %bitcast.6, ...), custom_call_target="tpu_custom_call" | custom-call | tf_op jit(solution)/shard_map/step/pallas_call | solution.py:304
  205.9 5.5 %put.1 = (bf16[2,640,1536]{2,1,0:T(8,128)(2,1)}, bf16[2,640,1536]{2,1,0:T(8,128)(2,1)}, bf16[2,1536,640]{2,1,0:T(8,128)(2,1)}, f32[2,80,1536]{2,1,0:T(8,128)}, f...) custom-call(bf16[2,640,1536]{2,1,0:T(8,128)(2,1)S(1)} %get-tuple-ele, ...), custom_call_target="tpu_custom_call" | custom-call | tf_op jit(solution)/shard_map/put/pallas_call | solution.py:317
  211.4 18.7 %last.1 = (bf16[2,3,80,1536]{3,2,1,0:T(8,128)(2,1)S(1)}, bf16[2,3,80,1536]{3,2,1,0:T(8,128)(2,1)S(1)}, bf16[2,3,192,640]{3,2,1,0:T(8,128)(2,1)S(1)}) custom-call(bf16[2,640,1536]{2,1,0:T(8,128)(2,1)S(1)} %get-tuple-element.33.refs_0_, bf16[2,640,1536]{2,1,0:T(8,128)(2,1)S(1)} %get-tuple-element.34.refs_1_, bf16[2,1536,640]{2,1,0:T(8,128)(2,1)S(1)} %get-tuple-element.35.refs_2_), custom_call_target="tpu_custom_call" | custom-call | tf_op jit(solution)/shard_map/last/pallas_call | solution.py:326
  230.1 1.4 put_last.1

commit v8 on v7

--- a/solution.py
+++ b/solution.py
@@ -215,15 +215,14 @@
             source = ring.new(w[a], layer, -way * (s - 1))
         b, *where = place(ring, c, way, s)
         if (c, way, s) in shared:
-            i = shared.index((c, way, s))
             side = source.shape[0] * 3 // 10 // 8 * 8
             rows = pl.ds(0, source.shape[0] - side) if (c, way, s) in late else pl.ds(source.shape[0] - side, side)
-            return ring.send(source.at[rows], out[b].at[*where, rows], send_sem.at[2 + i], recv_sem.at[i], way)
+            return ring.send(source.at[rows], out[b].at[*where, rows], send_sem.at[0], recv_sem.at[0], way)
         if (c, way, s + 1) in then:
-            i = 4 + then.index((c, way, s + 1))
+            i = 1 + then.index((c, way, s + 1))
         else:
-            i = 2 + WAYS.index(way)
-        return ring.send(source, out[b].at[*where], send_sem.at[int((c, way, s) in then)], recv_sem.at[i], way)
+            i = 0
+        return ring.send(source, out[b].at[*where], send_sem.at[0], recv_sem.at[i], way)
 
     @pl.when(ring.waits())
     def _():
@@ -234,13 +233,8 @@
             copy(c, way, s).start()
         for hop in shared:
             copy(*hop).start()
-        for i, way in enumerate(WAYS):
-            ends = [hop for hop in first + then if hop[1] == way and (*hop[:2], hop[2] + 1) not in then]
-            ring.done(w[0], len(ends), recv_sem.at[2 + i])
-        ring.done(w[0], len(first), send_sem.at[0])
-        ring.done(w[0], len(then), send_sem.at[1])
-        for hop in shared:
-            copy(*hop).wait()
+        ring.done(w[0], len(late) - len(then), recv_sem.at[0])
+        ring.done(w[0], len(late), send_sem.at[0])
 
 
 def put(ring, *refs):
@@ -329,7 +323,7 @@
             out_shape=[vmem(x) for x in ends],
             in_specs=spec(pltpu.VMEM, 3),
             out_specs=spec(pltpu.VMEM, 3),
-            scratch_shapes=[pltpu.SemaphoreType.DMA((4,)), pltpu.SemaphoreType.DMA((LATE + 4,))],
+            scratch_shapes=[pltpu.SemaphoreType.DMA((1,)), pltpu.SemaphoreType.DMA((LATE + 1,))],
             compiler_params=pltpu.CompilerParams(collective_id=1, has_side_effects=True, vmem_limit_bytes=20 << 20),
         )(*keep(pltpu.VMEM, out[:3]))
         whole = pl.pallas_call(

time: 232 us -> 232 us (level)
  no operation moved by 1% of the time
where the time goes in v8:
time: 232 us; the launch traced here: 231 us
  Pallas kernels  231 us (100%)
    pallas_call x1, Pallas kernels, step(): pl.pallas_call(lambda *refs: kernel(ring, *refs), name='step', out_shape=...  205 us
    pallas_call x1, Pallas kernels, step(): pl.pallas_call(lambda *refs: last(ring, *refs), name='last', out_shape=[v...  18.6 us
    pallas_call x1, Pallas kernels, step(): pl.pallas_call(lambda *refs: put(ring, *refs), name='put', out_shape=[hbm...  5.48 us

profile of v8, /device:TPU:22, one launch (start us, length us, event | category | flops | bytes accessed | tf_op | source)
XLA Modules:
  0.0 231.5 jit_solution(3949530718950348502)
XLA Ops:
  0.6 205.2 %step.1 = (bf16[2,640,1536]{2,1,0:T(8,128)(2,1)S(1)}, bf16[2,640,1536]{2,1,0:T(8,128)(2,1)S(1)}, bf16[2,1536,640]{2,1,0:T(8,128)(2,1)S(1)}, f32[2,80,1536]{2,1,0...) custom-call(bf16[2,8,80,1536]{3,2,1,0:T(8,128)(2,1)} %bitcast.6, ...), custom_call_target="tpu_custom_call" | custom-call | tf_op jit(solution)/shard_map/step/pallas_call | solution.py:298
  205.9 5.5 %put.1 = (bf16[2,640,1536]{2,1,0:T(8,128)(2,1)}, bf16[2,640,1536]{2,1,0:T(8,128)(2,1)}, bf16[2,1536,640]{2,1,0:T(8,128)(2,1)}, f32[2,80,1536]{2,1,0:T(8,128)}, f...) custom-call(bf16[2,640,1536]{2,1,0:T(8,128)(2,1)S(1)} %get-tuple-ele, ...), custom_call_target="tpu_custom_call" | custom-call | tf_op jit(solution)/shard_map/put/pallas_call | solution.py:311
  211.4 18.6 %last.1 = (bf16[2,3,80,1536]{3,2,1,0:T(8,128)(2,1)S(1)}, bf16[2,3,80,1536]{3,2,1,0:T(8,128)(2,1)S(1)}, bf16[2,3,192,640]{3,2,1,0:T(8,128)(2,1)S(1)}) custom-call(bf16[2,640,1536]{2,1,0:T(8,128)(2,1)S(1)} %get-tuple-element.33.refs_0_, bf16[2,640,1536]{2,1,0:T(8,128)(2,1)S(1)} %get-tuple-element.34.refs_1_, bf16[2,1536,640]{2,1,0:T(8,128)(2,1)S(1)} %get-tuple-element.35.refs_2_), custom_call_target="tpu_custom_call" | custom-call | tf_op jit(solution)/shard_map/last/pallas_call | solution.py:320
  230.0 1.4 put_last.1

commit v9 on v8

--- a/solution.py
+++ b/solution.py
@@ -233,8 +233,8 @@
             copy(c, way, s).start()
         for hop in shared:
             copy(*hop).start()
+        ring.done(w[0], len(late), send_sem.at[0])
         ring.done(w[0], len(late) - len(then), recv_sem.at[0])
-        ring.done(w[0], len(late), send_sem.at[0])
 
 
 def put(ring, *refs):

time: 232 us -> 232 us (level)
  no operation moved by 1% of the time
where the time goes in v9:
time: 232 us; the launch traced here: 231 us
  Pallas kernels  231 us (100%)
    pallas_call x1, Pallas kernels, step(): pl.pallas_call(lambda *refs: kernel(ring, *refs), name='step', out_shape=...  205 us
    pallas_call x1, Pallas kernels, step(): pl.pallas_call(lambda *refs: last(ring, *refs), name='last', out_shape=[v...  18.6 us
    pallas_call x1, Pallas kernels, step(): pl.pallas_call(lambda *refs: put(ring, *refs), name='put', out_shape=[hbm...  5.48 us

profile of v9, /device:TPU:22, one launch (start us, length us, event | category | flops | bytes accessed | tf_op | source)
XLA Modules:
  0.0 231.5 jit_solution(7246887455994664850)
XLA Ops:
  0.6 205.2 %step.1 = (bf16[2,640,1536]{2,1,0:T(8,128)(2,1)S(1)}, bf16[2,640,1536]{2,1,0:T(8,128)(2,1)S(1)}, bf16[2,1536,640]{2,1,0:T(8,128)(2,1)S(1)}, f32[2,80,1536]{2,1,0...) custom-call(bf16[2,8,80,1536]{3,2,1,0:T(8,128)(2,1)} %bitcast.6, ...), custom_call_target="tpu_custom_call" | custom-call | tf_op jit(solution)/shard_map/step/pallas_call | solution.py:298
  205.9 5.5 %put.1 = (bf16[2,640,1536]{2,1,0:T(8,128)(2,1)}, bf16[2,640,1536]{2,1,0:T(8,128)(2,1)}, bf16[2,1536,640]{2,1,0:T(8,128)(2,1)}, f32[2,80,1536]{2,1,0:T(8,128)}, f...) custom-call(bf16[2,640,1536]{2,1,0:T(8,128)(2,1)S(1)} %get-tuple-ele, ...), custom_call_target="tpu_custom_call" | custom-call | tf_op jit(solution)/shard_map/put/pallas_call | solution.py:311
  211.4 18.6 %last.1 = (bf16[2,3,80,1536]{3,2,1,0:T(8,128)(2,1)S(1)}, bf16[2,3,80,1536]{3,2,1,0:T(8,128)(2,1)S(1)}, bf16[2,3,192,640]{3,2,1,0:T(8,128)(2,1)S(1)}) custom-call(bf16[2,640,1536]{2,1,0:T(8,128)(2,1)S(1)} %get-tuple-element.33.refs_0_, bf16[2,640,1536]{2,1,0:T(8,128)(2,1)S(1)} %get-tuple-element.34.refs_1_, bf16[2,1536,640]{2,1,0:T(8,128)(2,1)S(1)} %get-tuple-element.35.refs_2_), custom_call_target="tpu_custom_call" | custom-call | tf_op jit(solution)/shard_map/last/pallas_call | solution.py:320
  230.0 1.4 put_last.1
